TPU v7x, 32 devices: a whole 2x2x4 slice. The times are simulated.
32 devices in a mesh: rep: 1, dp: 32 (over x, y, z, core).
Axes of the slice: x: 2, y: 2, z: 4, core: 2. Of those that a mesh axis runs over, the one named last changes fastest.
Arguments:
- g_w_gate: bfloat16 [32, 2, 1024, 3328], P(('rep', 'dp'))
- g_w_up: bfloat16 [32, 2, 1024, 3328], P(('rep', 'dp'))
- g_w_down: bfloat16 [32, 2, 3328, 1024], P(('rep', 'dp'))
- w_gate: bfloat16 [2, 1024, 3328], replicated
- w_up: bfloat16 [2, 1024, 3328], replicated
- w_down: bfloat16 [2, 3328, 1024], replicated
- m_w_gate: float32 [2, 1024, 3328], P(None, 'dp')
- m_w_up: float32 [2, 1024, 3328], P(None, 'dp')
- m_w_down: float32 [2, 3328, 1024], P(None, 'dp')
- v_w_gate: float32 [2, 1024, 3328], P(None, 'dp')
- v_w_up: float32 [2, 1024, 3328], P(None, 'dp')
- v_w_down: float32 [2, 3328, 1024], P(None, 'dp')
Outputs:
- output 1: bfloat16 [2, 1024, 3328], P('rep')
- output 2: bfloat16 [2, 1024, 3328], P('rep')
- output 3: bfloat16 [2, 3328, 1024], P('rep')
- output 4: float32 [2, 1024, 3328], P('rep', 'dp')
- output 5: float32 [2, 1024, 3328], P('rep', 'dp')
- output 6: float32 [2, 3328, 1024], P('rep', 'dp')
- output 7: float32 [2, 1024, 3328], P('rep', 'dp')
- output 8: float32 [2, 1024, 3328], P('rep', 'dp')
- output 9: float32 [2, 3328, 1024], P('rep', 'dp')
All inputs are finite; a program needn't handle non-finite values.
Results may differ from a plain program's by a relative error of at most 0.022.
Values are sent between devices in bfloat16 or wider.
A program may use at most 2 GiB of HBM per device.

v0:
```python
import jax
import jax.numpy as jnp
from jax import lax
from jax.sharding import PartitionSpec as P


def adamw(w, m, v, g):
    m = 0.9 * m + 0.1 * g
    v = 0.95 * v + 0.05 * g * g
    step = m * lax.rsqrt(v + 1e-8) + 0.1 * w
    return (w - 0.02 * step).astype(jnp.bfloat16), m, v


def clipped(gradients, sum_of_squares, count):
    factor = jnp.minimum(1.0, 0.5 * lax.rsqrt(sum_of_squares / count + 1e-30))
    return [g * factor for g in gradients]


def solution(mesh):
    def step(*arrays):
        terms, weights, m, v = (arrays[i : i + 3] for i in (0, 3, 6, 9))
        gradients = [lax.psum_scatter(t[0], "dp", scatter_dimension=1, tiled=True).astype(jnp.float32) for t in terms]
        squares = lax.psum(sum(jnp.sum(g * g) for g in gradients), "dp")
        gradients = clipped(gradients, squares, lax.psum(1, "dp") * sum(g.size for g in gradients))
        me = lax.axis_index("dp")
        own = [lax.dynamic_slice_in_dim(w, me * one.shape[1], one.shape[1], 1).astype(jnp.float32) for w, one in zip(weights, m, strict=True)]
        new = [adamw(w, m, v, g) for w, m, v, g in zip(own, m, v, gradients, strict=True)]
        whole = [lax.all_gather(one[0], "dp", axis=1, tiled=True) for one in new]
        return (*whole, *(one[1] for one in new), *(one[2] for one in new))

    all_of, cut = P(None, None, None), P(None, "dp", None)
    return jax.shard_map(
        step,
        mesh=mesh,
        in_specs=(P(("rep", "dp"), None, None, None),) * 3 + (all_of,) * 3 + (cut,) * 6,
        out_specs=(P("rep", None, None),) * 3 + (P("rep", "dp", None),) * 6,
        check_vma=False,
    )
```

profile of v0, /device:TPU:0, one launch (start us, length us, event | category | flops | bytes accessed | tf_op | source)
XLA Modules:
  0.0 925.9 jit_solution(14436476276501451551)
XLA Ops:
  7.2 0.0 reduce-scatter.10.cloned.1.call-start
  7.2 22.9 %copy.21 = bf16[2,3328,1024]{2,0,1:T(2,128)(2,1)S(1)} copy(bf16[2,3328,1024]{2,1,0:T(8,128)(2,1)} %bitcast.9) | data formatting | bytes 27262976
  30.1 7.8 copy.23
  38.0 0.0 reduce-scatter.10.cloned.1.call-update
  38.0 0.0 reduce-scatter.6.cloned.1.call-start
  38.1 0.0 copy-start.1
  38.1 0.0 copy-start.2
  38.1 0.7 reduce-scatter.6.cloned.1.call-update
  38.8 0.0 copy-start.3
  38.8 0.0 reduce-scatter.8.cloned.1.call-start
  38.8 0.7 reduce-scatter.8.cloned.1.call-update
  39.5 0.0 all-gather.8.cloned.1.call-start
  39.6 168.2 %reduce-scatter.10.cloned.1.call-done = bf16[104,2048]{1,0:T(8,128)(2,1)} async-done(((bf16[3328,2048]{1,0:T(8,128)(2,1)}), bf16[104,2048]{1,0:T(8,128)(2,1)}) %reduce-scatter.10.cloned.1.call-update) | async-done | bytes 426000
  207.8 1.3 reshape.19
  209.1 166.2 %reduce-scatter.6.cloned.1.call-done = bf16[2,32,3328]{2,1,0:T(8,128)(2,1)} async-done(((bf16[2,1024,3328]{2,1,0:T(8,128)(2,1)}), bf16[2,32,3328]{2,1,0:T(8,128)(2,1)}) %reduce-scatter.6.cloned.1.call-update) | async-done | bytes 426000 | tf_op jit(solution)/shard_map/reduce_scatter | solution.py:22
  375.3 1.8 fusion.9
  377.1 0.8 fusion.11
  378.0 164.5 %reduce-scatter.8.cloned.1.call-done = bf16[2,32,3328]{2,1,0:T(8,128)(2,1)} async-done(((bf16[2,1024,3328]{2,1,0:T(8,128)(2,1)}), bf16[2,32,3328]{2,1,0:T(8,128)(2,1)}) %reduce-scatter.8.cloned.1.call-update) | async-done | bytes 426000 | tf_op jit(solution)/shard_map/reduce_scatter | solution.py:22
  542.5 1.8 fusion.10
  546.2 36.9 %psum.7 = f32[]{:T(128)} all-reduce(f32[]{:T(128)S(6)} %add.65), channel_id=1, replica_groups=mesh['rep'=1,'dp'=32] {'dp'}, use_global_device_ids=true, to_apply=%region_6.0 | all-reduce | flops 1 | bytes 8 | tf_op jit(solution)/shard_map/psum | solution.py:23
  583.8 0.0 copy-done.1
  583.8 0.0 copy-done.2
  583.8 2.6 fusion.17
  586.4 0.0 all-gather.8.cloned.1.call-update
  586.5 0.0 all-gather.4.cloned.1.call-start
  586.5 0.0 copy-done.3
  586.5 3.0 fusion.8
  589.5 0.0 all-gather.4.cloned.1.call-update
  589.5 0.0 all-gather.6.cloned.1.call-start
  589.6 3.2 fusion.14
  592.8 0.0 all-gather.6.cloned.1.call-update
  592.8 95.4 %all-gather.8.cloned.1.call-done = bf16[2,3328,1024]{2,1,0:T(8,128)(2,1)} async-done(((bf16[2,104,1024]{2,1,0:T(8,128)(2,1)}), bf16[2,3328,1024]{2,1,0:T(8,128)(2,1)}) %all-gather.8.cloned.1.call-update) | async-done | bytes 13631504 | tf_op jit(solution)/shard_map/all_gather | solution.py:28
  688.2 101.8 %all-gather.4.cloned.1.call-done = bf16[2,1024,3328]{2,1,0:T(8,128)(2,1)} async-done(((bf16[2,32,3328]{2,1,0:T(8,128)(2,1)}), bf16[2,1024,3328]{2,1,0:T(8,128)(2,1)}) %all-gather.4.cloned.1.call-update) | async-done | bytes 13631504 | tf_op jit(solution)/shard_map/all_gather | solution.py:28
  790.0 101.8 %all-gather.6.cloned.1.call-done = bf16[2,1024,3328]{2,1,0:T(8,128)(2,1)} async-done(((bf16[2,32,3328]{2,1,0:T(8,128)(2,1)}), bf16[2,1024,3328]{2,1,0:T(8,128)(2,1)}) %all-gather.6.cloned.1.call-update) | async-done | bytes 13631504 | tf_op jit(solution)/shard_map/all_gather | solution.py:28
  891.8 0.0 copy-start
  891.8 0.0 slice-start
  891.8 0.0 slice-start.1
  891.8 15.1 %copy.32 = bf16[2,1024,3328]{2,1,0:T(8,128)(2,1)} copy(bf16[2,1024,3328]{2,1,0:T(8,128)(2,1)} %all-gather.4.cloned.1.call-done) | data formatting | bytes 27262976
  906.9 0.0 copy-done
  906.9 0.0 slice-start.2
  906.9 0.0 slice-start.3
  906.9 6.6 copy.33
  913.4 0.0 slice-done
  913.4 0.0 slice-done.1
  913.4 0.0 slice-done.2
  913.4 0.5 slice-done.3
  913.9 5.1 copy.34
  (1 shorter events, 0.0 us)
Async XLA Ops:
  7.2 200.6 %reduce-scatter.10.cloned.1.call-start = ((), (), s32[]{:S(2)}) async-start(), calls=%async_computation.8 | async-start | bytes 14057472
  38.0 337.3 %reduce-scatter.6.cloned.1.call-start = ((), (), s32[]{:S(2)}) async-start(), calls=%async_computation.3 | async-start | bytes 14057472 | tf_op jit(solution)/shard_map/reduce_scatter | solution.py:22
  38.1 545.8 %copy-start.1 = (f32[2,104,1024]{2,1,0:T(8,128)S(1)}, f32[2,104,1024]{2,1,0:T(8,128)}, u32[]{:S(2)}) copy-start(f32[2,104,1024]{2,1,0:T(8,128)} %param.23) | copy-start | bytes 2555908
  38.1 545.8 %copy-start.2 = (f32[2,104,1024]{2,1,0:T(8,128)S(1)}, f32[2,104,1024]{2,1,0:T(8,128)}, u32[]{:S(2)}) copy-start(f32[2,104,1024]{2,1,0:T(8,128)} %param.20) | copy-start | bytes 2555908
  38.8 547.8 %copy-start.3 = (f32[2,32,3328]{2,1,0:T(8,128)S(1)}, f32[2,32,3328]{2,1,0:T(8,128)}, u32[]{:S(2)}) copy-start(f32[2,32,3328]{2,1,0:T(8,128)} %param.21) | copy-start | bytes 2555908
  38.8 503.7 %reduce-scatter.8.cloned.1.call-start = ((), (), s32[]{:S(2)}) async-start(), calls=%async_computation.4 | async-start | bytes 14057472 | tf_op jit(solution)/shard_map/reduce_scatter | solution.py:22
  39.5 648.6 %all-gather.8.cloned.1.call-start = ((), (), s32[]{:S(2)}) async-start(), calls=%async_computation.7 | async-start | bytes 14057472 | tf_op jit(solution)/shard_map/all_gather | solution.py:28
  586.5 203.5 %all-gather.4.cloned.1.call-start = ((), (), s32[]{:S(2)}) async-start(), calls=%async_computation.5 | async-start | bytes 14057472 | tf_op jit(solution)/shard_map/all_gather | solution.py:28
  589.5 302.3 %all-gather.6.cloned.1.call-start = ((), (), s32[]{:S(2)}) async-start(), calls=%async_computation.6 | async-start | bytes 14057472 | tf_op jit(solution)/shard_map/all_gather | solution.py:28
  891.8 15.1 %copy-start = (bf16[2,1024,3328]{2,1,0:T(8,128)(2,1)S(1)}, bf16[2,1024,3328]{2,1,0:T(8,128)(2,1)}, u32[]{:S(2)}) copy-start(bf16[2,1024,3328]{2,1,0:T(8,128)(2,1)} %all-gather.6.cloned.1.call-done) | copy-start | bytes 40894468
  891.8 21.6 %slice-start = ((s8[13631488]{0:T(1024)(128)(4,1)}), s8[4194304]{0:T(1024)(128)(4,1)S(1)}, s32[]{:S(2)}) async-start(s8[13631488]{0:T(1024)(128)(4,1)} %bitcast.12), calls=%async_computation.9 | async-start | bytes 8388608
  891.8 21.6 %slice-start.1 = ((s8[13631488]{0:T(1024)(128)(4,1)}), s8[4194304]{0:T(1024)(128)(4,1)S(1)}, s32[]{:S(2)}) async-start(s8[13631488]{0:T(1024)(128)(4,1)} %bitcast.12), calls=%async_computation.10 | async-start | bytes 8388608
  906.9 6.6 slice-start.2
  906.9 7.1 slice-start.3
Sparse Core Ops, SparseCore 0:
  38.1 169.6 reduce-scatter.9
  210.1 165.1 reduce-scatter.5
  377.6 164.7 reduce-scatter.7
  586.6 101.5 all-gather.7
  691.5 98.4 all-gather.3
  793.3 98.4 all-gather.5
where the time goes:
time: 926 us
  waiting for transfers between devices  799 us (86%)
  local copies, waits for them, and re-layouts  59.4 us (6%)
  blocking collectives  36.9 us (4%)
  between operations  16.8 us (2%)
  other arithmetic  13.3 us (1%)
    reduce_scatter x2, waiting for transfers between devices, step(): lax.psum_scatter(t[0], 'dp', scatter_dimension=1, tiled=True)  331 us
    all_gather x3, waiting for transfers between devices, step(): whole = [lax.all_gather(one[0], 'dp', axis=1, tiled=True) for one in new]  299 us
    unnamed x7, waiting for transfers between devices  170 us
    unnamed x22, local copies, waits for them, and re-layouts  59.4 us
    psum x1, blocking collectives, step(): squares = lax.psum(sum((jnp.sum(g * g) for g in gradients)), 'dp')  36.9 us
  transfers between devices with their start and end apart: 6, of which 6 were waited for; matrix products, arithmetic and copies ran while one was open for 1% of the time, Pallas kernels for 0%

commit v1 on v0

v1 whole, which is shorter than its diff:
```python
import functools

import jax
import jax.numpy as jnp
from jax import lax
from jax.experimental import pallas as pl
from jax.experimental.pallas import tpu as pltpu
from jax.sharding import PartitionSpec as P

MESH = pl.DeviceIdType.MESH
CHIPS = 16
TILES, PART = 52, 13
ROUNDS = 12
START, COUNT = (0, 8, 12, 14), (8, 4, 2, 1)
SUM_LAG = (0, 1, 2, 3, 4)
GATHER_LAG = (0, 1, 2, 3, 4)


def view(t):
    layers, rows, columns = t.shape
    return t.reshape(layers, rows // 8, 8, columns // 128, 128).transpose(0, 1, 3, 2, 4).reshape(layers, -1, TILES, 16, 128)


def unview(t, shape):
    layers, rows, columns = shape
    return t.reshape(layers, rows // 8, columns // 128, 8, 128).transpose(0, 1, 3, 2, 4).reshape(shape)


def place():
    me = lax.axis_index("dp")
    return me, me // 2, me % 2


def is_down(t):
    return (t % 3) // 2


def source(t):
    i = 2 * (t // 3) + t % 3
    return i // 4, i % 4, t // 3


def bits(t, a):
    d = is_down(t)
    first, last = (8, 4) if a == 0 else (4, 8)
    return first, 1 + (last - 1) * d, 2 - d, last - (last - 2) * d


def bit(k, b):
    return (k // b) % 2


def flip(k, b):
    return k + (1 - 2 * bit(k, b)) * b


def copy_to(src, dst, send, recv, chip, core):
    return pltpu.make_async_remote_copy(src_ref=src, dst_ref=dst, send_sem=send, recv_sem=recv, device_id={"dp": 2 * chip + core}, device_id_type=MESH)


def sum_kernel(gate, up, down, out, norm, own, pair, slots, squares, parts, own_sem, pair_send, pair_recv, send, recv, norm_send, norm_recv):
    me, k, c = place()

    def arrays(t, a, core):
        if t % 3 == 2:
            return down.at[a, :, core, pl.ds(source(t)[2] * PART, PART)]
        layer, part, _ = source(t)
        return (gate, up)[a].at[layer, :, core, pl.ds(part * PART, PART)]

    for t in range(ROUNDS):
        for a in range(2):
            copy_to(arrays(t, a, 1 - c), pair.at[t, a], pair_send.at[t, a], pair_recv.at[t, a], k, 1 - c).start()
            pltpu.make_async_copy(arrays(t, a, c), own.at[t, a], own_sem.at[t, a]).start()
    squares[...] = jnp.zeros_like(squares)

    def await_slots(t, a, s):
        got = slots.at[t, a, pl.ds(START[s], COUNT[s])]
        pltpu.make_async_copy(got, got, recv.at[t, a, s]).wait()

    def total(t, a, s, chip):
        b = bits(t, a)
        so_far = own[t, a, chip].astype(jnp.float32) + pair[t, a, chip].astype(jnp.float32)
        for i in range(s):
            index = START[i]
            for j in range(i + 1, 4):
                index = index + bit(chip, b[j]) * 2 ** (3 - j)
            so_far = so_far + slots[t, a, index].astype(jnp.float32)
        return so_far

    def stage(t, a, s):
        b = bits(t, a)
        other = flip(k, b[s])
        if s == 0:
            pltpu.make_async_copy(own.at[t, a], own.at[t, a], own_sem.at[t, a]).wait()
            pltpu.make_async_copy(pair.at[t, a], pair.at[t, a], pair_recv.at[t, a]).wait()
        else:
            await_slots(t, a, s - 1)
        base = other
        for i in range(s + 1, 4):
            base = base - bit(other, b[i]) * b[i]

        def chip_of(j):
            chip = base
            for i in range(s + 1, 4):
                chip = chip + bit(j, 2 ** (3 - i)) * b[i]
            return chip

        def add(j, _):
            chip = chip_of(j)
            own[t, a, chip] = total(t, a, s, chip).astype(jnp.bfloat16)
            return 0

        def go(j, _):
            copy_to(own.at[t, a, chip_of(j)], slots.at[t, a, START[s] + j], send.at[t, a, s], recv.at[t, a, s], other, c).start()
            return 0

        lax.fori_loop(0, COUNT[s], add, 0)
        lax.fori_loop(0, COUNT[s], go, 0)

    def finish(t, a):
        await_slots(t, a, 3)
        g = total(t, a, 4, k).astype(jnp.bfloat16)
        out[t, a] = g
        g = g.astype(jnp.float32)
        squares[...] += jnp.sum(g * g, axis=0)

    def step(now, _):
        for s in range(5):
            t = now - SUM_LAG[s]

            @pl.when((t >= 0) & (t < ROUNDS))
            def _():
                for a in range(2):
                    if s < 4:
                        stage(t, a, s)
                    else:
                        finish(t, a)

        return 0

    lax.fori_loop(0, ROUNDS + SUM_LAG[4], step, 0)

    mine = parts.at[me]
    mine[...] = squares[...]

    def tell(i, _):
        to = (me + i) % 32
        pltpu.make_async_remote_copy(src_ref=squares, dst_ref=mine, send_sem=norm_send, recv_sem=norm_recv, device_id={"dp": to}, device_id_type=MESH).start()
        return 0

    lax.fori_loop(1, 32, tell, 0)
    others = parts.at[pl.ds(0, 31)]
    pltpu.make_async_copy(others, others, norm_recv).wait()
    norm[...] = jnp.sum(parts[...], axis=0)
    pltpu.make_async_copy(others, others, norm_send).wait()

    def drain(t, _):
        for a in range(2):
            pltpu.make_async_copy(pair.at[t, a], pair.at[t, a], pair_send.at[t, a]).wait()
            for s in range(4):
                sent = slots.at[t, a, pl.ds(START[s], COUNT[s])]
                pltpu.make_async_copy(sent, sent, send.at[t, a, s]).wait()
        return 0

    lax.fori_loop(0, ROUNDS, drain, 0)


def gather_kernel(new, gate, up, down, own_sem, pair_send, pair_recv, send, recv):
    _, k, c = place()

    def block(t, a, chip, core, count=None):
        chip = chip if count is None else pl.ds(chip, count)
        if t % 3 == 2:
            return down.at[a, chip, core, pl.ds(source(t)[2] * PART, PART)]
        layer, part, _ = source(t)
        return (gate, up)[a].at[layer, chip, core, pl.ds(part * PART, PART)]

    for t in range(ROUNDS):
        for a in range(2):
            pltpu.make_async_copy(new.at[t, a], block(t, a, k, c), own_sem.at[t, a]).start()

    def chips(t, a, s, at):
        b = bits(t, a)[::-1]
        base = at
        for i in range(s):
            base = base - bit(at, b[i]) * b[i]

        def chip_of(j):
            chip = base
            for i in range(s):
                chip = chip + bit(j, 2**i) * b[i]
            return chip

        return chip_of

    def whole(t, a, count):
        return block(t, a, 0, 0, count)

    def pass_on(t, a, s):
        if s == 0:
            of, count = chips(t, a, 0, k), 1
        else:
            of, count = chips(t, a, s - 1, flip(k, bits(t, a)[4 - s])), 2 ** (s - 1)

        def go(j, _):
            one = block(t, a, of(j), c)
            copy_to(one, one, pair_send.at[t, a], pair_recv.at[t, a], k, 1 - c).start()
            return 0

        lax.fori_loop(0, count, go, 0)

    def stage(t, a, s):
        if s == 0:
            pltpu.make_async_copy(new.at[t, a], new.at[t, a], own_sem.at[t, a]).wait()
        else:
            got = whole(t, a, 2 ** (s - 1))
            pltpu.make_async_copy(got, got, recv.at[t, a, s - 1]).wait()
        if s < 4:
            of, other = chips(t, a, s, k), flip(k, bits(t, a)[3 - s])

            def go(j, _):
                one = block(t, a, of(j), c)
                copy_to(one, one, send.at[t, a, s], recv.at[t, a, s], other, c).start()
                return 0

            lax.fori_loop(0, 2**s, go, 0)
        pass_on(t, a, s)

    for now in range(ROUNDS + GATHER_LAG[4]):
        for s in range(5):
            t = now - GATHER_LAG[s]
            if 0 <= t < ROUNDS:
                for a in range(2):
                    stage(t, a, s)

    for t in range(ROUNDS):
        for a in range(2):
            pltpu.make_async_copy(whole(t, a, 16), whole(t, a, 16), pair_recv.at[t, a]).wait()
            pltpu.make_async_copy(whole(t, a, 16), whole(t, a, 16), pair_send.at[t, a]).wait()
            for s in range(4):
                pltpu.make_async_copy(whole(t, a, 2**s), whole(t, a, 2**s), send.at[t, a, s]).wait()


def adamw(w, m, v, g):
    m = 0.9 * m + 0.1 * g
    v = 0.95 * v + 0.05 * g * g
    step = m * lax.rsqrt(v + 1e-8) + 0.1 * w
    return (w - 0.02 * step).astype(jnp.bfloat16), m, v


def split(rounds):
    rounds = rounds.reshape(4, 3, 2, PART, 16, 128)
    sides = rounds[:, :2].reshape(2, 4, 2, PART, 16, 128)
    gate, up = (sides[:, :, a].reshape(2, TILES, 16, 128) for a in range(2))
    return gate, up, jnp.swapaxes(rounds[:, 2], 0, 1).reshape(2, TILES, 16, 128)


def merge(gate, up, down):
    sides = jnp.stack([one.reshape(8, PART, 16, 128) for one in (gate, up)], 1).reshape(4, 2, 2, PART, 16, 128)
    down = jnp.swapaxes(down.reshape(2, 4, PART, 16, 128), 0, 1)
    return jnp.concatenate([sides, down[:, None]], 1).reshape(ROUNDS, 2, PART, 16, 128)


def solution(mesh):
    hbm, vmem = pl.BlockSpec(memory_space=pl.ANY), pl.BlockSpec(memory_space=pltpu.VMEM)
    dma = pltpu.SemaphoreType.DMA
    params = pltpu.CompilerParams(has_side_effects=True, vmem_limit_bytes=67043328)

    def step(*arrays):
        terms, weights, m, v = (arrays[i : i + 3] for i in (0, 3, 6, 9))
        tile = (16, 128)
        terms = [view(t[0]).reshape(2, CHIPS, 2, TILES, *tile) for t in terms]
        summed, norm = pl.pallas_call(
            sum_kernel,
            out_shape=[jax.ShapeDtypeStruct((ROUNDS, 2, PART, *tile), jnp.bfloat16), jax.ShapeDtypeStruct(tile, jnp.float32)],
            in_specs=[hbm] * 3,
            out_specs=[vmem] * 2,
            scratch_shapes=[
                pltpu.VMEM((ROUNDS, 2, CHIPS, PART, *tile), jnp.bfloat16),
                pltpu.VMEM((ROUNDS, 2, CHIPS, PART, *tile), jnp.bfloat16),
                pltpu.VMEM((ROUNDS, 2, 15, PART, *tile), jnp.bfloat16),
                pltpu.VMEM(tile, jnp.float32),
                pltpu.VMEM((32, *tile), jnp.float32),
                dma((ROUNDS, 2)),
                dma((ROUNDS, 2)),
                dma((ROUNDS, 2)),
                dma((ROUNDS, 2, 4)),
                dma((ROUNDS, 2, 4)),
                dma,
                dma,
            ],
            compiler_params=params,
        )(*terms)
        count = 32 * sum(one.size for one in m)
        factor = jnp.minimum(1.0, 0.5 * lax.rsqrt(jnp.sum(norm) / count + 1e-30))
        me = lax.axis_index("dp")
        own = [lax.dynamic_index_in_dim(view(w), me, 1, False).astype(jnp.float32) for w in weights]
        g = [one.astype(jnp.float32) * factor for one in split(summed)]
        new = [adamw(w, view(m)[:, 0], view(v)[:, 0], g) for w, m, v, g in zip(own, m, v, g, strict=True)]
        whole = pl.pallas_call(
            gather_kernel,
            out_shape=[jax.ShapeDtypeStruct((2, CHIPS, 2, TILES, *tile), jnp.bfloat16)] * 3,
            in_specs=[vmem],
            out_specs=[hbm] * 3,
            scratch_shapes=[
                dma((ROUNDS, 2)),
                dma((ROUNDS, 2)),
                dma((ROUNDS, 2)),
                dma((ROUNDS, 2, 4)),
                dma((ROUNDS, 2, 4)),
            ],
            compiler_params=params,
        )(merge(*(one[0] for one in new)))
        whole = [unview(one, w.shape) for one, w in zip(whole, weights, strict=True)]
        return (*whole, *(unview(n[1], one.shape) for n, one in zip(new, m, strict=True)), *(unview(n[2], one.shape) for n, one in zip(new, v, strict=True)))

    all_of, cut = P(None, None, None), P(None, "dp", None)
    return jax.shard_map(
        step,
        mesh=mesh,
        in_specs=(P(("rep", "dp"), None, None, None),) * 3 + (all_of,) * 3 + (cut,) * 6,
        out_specs=(P("rep", None, None),) * 3 + (P("rep", "dp", None),) * 6,
        check_vma=False,
    )
```

time: 926 us -> 412 us (0.44)
  waiting for transfers between devices: 799 us -> 0 us
  Pallas kernels: 0 us -> 362 us
  blocking collectives: 36.9 us -> 0 us
  local copies, waits for them, and re-layouts: 59.4 us -> 29.2 us
  between operations: 16.8 us -> 1.55 us
    pallas_call x0 -> x2, Pallas kernels: none -> 362 us  [the longest x1 182 us: step(): pl.pallas_call(sum_kernel, out_shape=[jax.ShapeDtypeStruct((ROUNDS, 2, PA...]
    reduce_scatter x2 -> x0, waiting for transfers between devices: 331 us -> none  [step(): lax.psum_scatter(t[0], 'dp', scatter_dimension=1, tiled=True)]
    all_gather x3 -> x0, waiting for transfers between devices: 299 us -> none  [step(): whole = [lax.all_gather(one[0], 'dp', axis=1, tiled=True) for one in new]]
    unnamed x7 -> x0, waiting for transfers between devices: 170 us -> none
    psum x1 -> x0, blocking collectives: 36.9 us -> none  [step(): squares = lax.psum(sum((jnp.sum(g * g) for g in gradients)), 'dp')]
    unnamed x22 -> x27, local copies, waits for them, and re-layouts: 59.4 us -> 23.9 us
  transfers between devices with their start and end apart: 6 -> 0, of which waited for: 6 -> 0; matrix products, arithmetic and copies ran while one was open for 1% -> 0% of each run, Pallas kernels for 0% -> 0%
where the time goes in v1:
time: 412 us
  Pallas kernels  362 us (88%)
  local copies, waits for them, and re-layouts  29.2 us (7%)
  other arithmetic  18.7 us (5%)
    pallas_call x1, Pallas kernels, step(): pl.pallas_call(sum_kernel, out_shape=[jax.ShapeDtypeStruct((ROUNDS, 2, PA...  182 us
    pallas_call x1, Pallas kernels, step(): pl.pallas_call(gather_kernel, out_shape=[jax.ShapeDtypeStruct((2, CHIPS,...  180 us
    unnamed x27, local copies, waits for them, and re-layouts  23.9 us

profile of v1, /device:TPU:0, one launch (start us, length us, event | category | flops | bytes accessed | tf_op | source)
XLA Modules:
  0.0 411.6 jit_solution(10771775693419989625)
XLA Ops:
  0.6 181.8 %shard_map.187 = (bf16[12,2,13,16,128]{4,3,2,1,0:T(8,128)(2,1)}, f32[16,128]{1,0:T(8,128)}) custom-call(bf16[2,16,2,52,16,128]{5,4,3,2,1,0:T(8,128)(2,1)} %bitcast.153, bf16[2,16,2,52,16,128]{5,4,3,2,1,0:T(8,128)(2,1)} %bitcast.154, bf16[2,16,2,52,16,128]{5,4,3,2,1,0:T(8,128)(2,1)} %bitcast.155), custom_call_target="tpu_custom_call" | custom-call | tf_op jit(solution)/shard_map/pallas_call | solution.py:273
  182.5 0.0 copy-start.4
  182.5 0.0 copy-start.5
  182.5 2.3 slice.16
  184.8 1.3 reduce_sum.9
  186.8 1.3 convert_multiply_fusion.5
  188.1 0.0 copy-start.2
  188.1 0.0 copy-start.3
  188.1 0.0 copy-start.7
  188.1 0.0 copy-start.6
  188.2 1.9 constant_dynamic-slice_fusion
  190.1 1.2 broadcast_multiply_fusion.4
  191.3 1.2 broadcast_multiply_fusion.2
  192.5 0.4 fusion.5
  193.0 1.0 constant_dynamic-slice_fusion.2
  194.0 0.0 copy-done.4
  194.0 0.1 broadcast_multiply_fusion.3
  194.1 0.0 copy-done.5
  194.1 0.1 broadcast_multiply_fusion.5
  194.2 0.0 copy-done.2
  194.2 0.4 fusion.2
  194.6 0.0 copy-done.3
  194.6 0.0 copy-done.7
  194.6 0.1 broadcast_multiply_fusion.1
  194.8 0.0 copy-done.6
  194.8 0.1 broadcast_multiply_fusion
  194.9 1.5 fusion.31
  196.3 1.3 pad_maximum_fusion
  197.6 180.4 %shard_map.188 = (bf16[2,16,2,52,16,128]{5,4,3,2,1,0:T(8,128)(2,1)}, bf16[2,16,2,52,16,128]{5,4,3,2,1,0:T(8,128)(2,1)}, bf16[2,16,2,52,16,128]{5,4,3,2,1,0:T(8,128)(2,1)}) custom-call(bf16[12,2,13,16,128]{4,3,2,1,0:T(8,128)(2,1)} %bitcast.165), custom_call_target="tpu_custom_call" | custom-call | tf_op jit(solution)/shard_map/pallas_call | solution.py:300
  378.0 0.0 copy-start.1
  378.0 4.6 %fusion.22 = (f32[2,32,3328]{2,1,0:T(8,128)}, f32[2,32,3328]{2,1,0:T(8,128)}, f32[2,32,3328]{2,1,0:T(8,128)}, f32[2,32,3328]{2,1,0:T(8,128)}) fusion(f32[2,4,26,8,128]{4,3,2,1,0:T(8,128)} %bitcast.162, f32[2,32,3328]{2,1,0:T(8,128)} %param.21, f32[2,32,3328]{2,1,0:T(8,128)} %param.18, f32[2,4,26,8,128]{4,3,2,1,0:T(8,128)} %bitcast.164, ...), kind=kLoop, calls=%fused_computation.35 | loop fusion | flops 2981888 | bytes 8519680 | tf_op jit(solution)/shard_map/reshape | solution.py:26
  382.5 1.8 convert_multiply_fusion.3
  384.4 3.3 fusion.26
  387.7 0.0 copy-done.1
  387.7 0.0 copy-start
  387.7 0.0 slice-start
  387.7 0.0 slice-start.1
  387.7 0.0 slice-start.2
  387.7 6.9 %copy.51 = bf16[2,1024,3328]{2,1,0:T(8,128)(2,1)} copy(bf16[2,1024,3328]{2,1,0:T(8,128)(2,1)S(1)} %bitcast.160) | data formatting | bytes 27262976
  394.6 2.9 copy-done
  397.5 0.0 slice-start.3
  397.5 6.9 %copy.52 = bf16[2,1024,3328]{2,1,0:T(8,128)(2,1)} copy(bf16[2,1024,3328]{2,1,0:T(8,128)(2,1)S(1)} %bitcast.159) | data formatting | bytes 27262976
  404.4 0.0 slice-done
  404.4 0.0 slice-done.1
  404.4 1.6 slice-done.2
  406.0 0.5 slice-done.3
  406.5 5.1 %copy.53 = bf16[2,3328,1024]{2,1,0:T(8,128)(2,1)} copy(bf16[2,3328,1024]{2,1,0:T(8,128)(2,1)S(1)} %bitcast.158) | data formatting | bytes 27262976
  (1 shorter events, 0.0 us)
Async XLA Ops:
  182.5 11.6 %copy-start.4 = (f32[2,32,3328]{2,1,0:T(8,128)S(1)}, f32[2,32,3328]{2,1,0:T(8,128)}, u32[]{:S(2)}) copy-start(f32[2,32,3328]{2,1,0:T(8,128)} %param.21) | copy-start | bytes 2555908
  182.5 11.6 %copy-start.5 = (f32[2,32,3328]{2,1,0:T(8,128)S(1)}, f32[2,32,3328]{2,1,0:T(8,128)}, u32[]{:S(2)}) copy-start(f32[2,32,3328]{2,1,0:T(8,128)} %param.18) | copy-start | bytes 2555908
  188.1 6.1 %copy-start.2 = (f32[2,4,1,13,16,128]{5,4,3,1,0,2:T(8,128)}, f32[2,4,1,13,16,128]{5,4,3,1,0,2:T(8,128)S(1)}, u32[]{:S(2)}) copy-start(f32[2,4,1,13,16,128]{5,4,3,1,0,2:T(8,128)S(1)} %get-tuple-element.25) | copy-start | bytes 2555908
  188.1 6.5 %copy-start.3 = (f32[2,4,1,13,16,128]{5,4,3,1,0,2:T(8,128)}, f32[2,4,1,13,16,128]{5,4,3,1,0,2:T(8,128)S(1)}, u32[]{:S(2)}) copy-start(f32[2,4,1,13,16,128]{5,4,3,1,0,2:T(8,128)S(1)} %get-tuple-element.26) | copy-start | bytes 2555908
  188.1 6.5 %copy-start.7 = (f32[2,104,1024]{2,1,0:T(8,128)S(1)}, f32[2,104,1024]{2,1,0:T(8,128)}, u32[]{:S(2)}) copy-start(f32[2,104,1024]{2,1,0:T(8,128)} %param.20) | copy-start | bytes 2555908
  188.1 6.6 %copy-start.6 = (f32[2,104,1024]{2,1,0:T(8,128)S(1)}, f32[2,104,1024]{2,1,0:T(8,128)}, u32[]{:S(2)}) copy-start(f32[2,104,1024]{2,1,0:T(8,128)} %param.23) | copy-start | bytes 2555908
  378.0 9.7 %copy-start.1 = (bf16[2,16,2,52,16,128]{5,4,3,2,1,0:T(8,128)(2,1)S(1)}, bf16[2,16,2,52,16,128]{5,4,3,2,1,0:T(8,128)(2,1)}, u32[]{:S(2)}) copy-start(bf16[2,16,2,52,16,128]{5,4,3,2,1,0:T(8,128)(2,1)} %get-tuple-element.16) | copy-start | bytes 40894468
  387.7 9.8 %copy-start = (bf16[2,16,2,52,16,128]{5,4,3,2,1,0:T(8,128)(2,1)S(1)}, bf16[2,16,2,52,16,128]{5,4,3,2,1,0:T(8,128)(2,1)}, u32[]{:S(2)}) copy-start(bf16[2,16,2,52,16,128]{5,4,3,2,1,0:T(8,128)(2,1)} %get-tuple-element.17) | copy-start | bytes 40894468
  387.7 16.7 %slice-start = ((s8[13631488]{0:T(1024)(128)(4,1)}), s8[4194304]{0:T(1024)(128)(4,1)S(1)}, s32[]{:S(2)}) async-start(s8[13631488]{0:T(1024)(128)(4,1)} %bitcast.156), calls=%async_computation | async-start | bytes 8388608
  387.7 16.7 %slice-start.1 = ((s8[13631488]{0:T(1024)(128)(4,1)}), s8[4194304]{0:T(1024)(128)(4,1)S(1)}, s32[]{:S(2)}) async-start(s8[13631488]{0:T(1024)(128)(4,1)} %bitcast.156), calls=%async_computation.1 | async-start | bytes 8388608
  387.7 18.3 %slice-start.2 = ((s8[13631488]{0:T(1024)(128)(4,1)}), s8[4194304]{0:T(1024)(128)(4,1)S(1)}, s32[]{:S(2)}) async-start(s8[13631488]{0:T(1024)(128)(4,1)} %bitcast.156), calls=%async_computation.2 | async-start | bytes 8388608
  397.5 9.0 %slice-start.3 = ((s8[13631488]{0:T(1024)(128)(4,1)}), s8[1048576]{0:T(1024)(128)(4,1)S(1)}, s32[]{:S(2)}) async-start(s8[13631488]{0:T(1024)(128)(4,1)} %bitcast.156), calls=%async_computation.3 | async-start | bytes 2097152

commit v2 on v1

v2 whole, which is shorter than its diff:
```python
import functools

import jax
import jax.numpy as jnp
from jax import lax
from jax.experimental import pallas as pl
from jax.experimental.pallas import tpu as pltpu
from jax.sharding import PartitionSpec as P

MESH = pl.DeviceIdType.MESH
CHIPS = 16
ROWS, TILES, PART = 8, 104, 13
PARTS = TILES // PART
ROUNDS = 3 * PARTS
START, COUNT = (0, 8, 12, 14), (8, 4, 2, 1)
AHEAD = 3
SUM_LAG = (0, 1, 2, 3, 4)
GATHER_LAG = (0, 1, 2, 3, 4)


def view(t):
    layers, rows, columns = t.shape
    return t.reshape(layers, rows // 8, 8, columns // 128, 128).transpose(0, 1, 3, 2, 4).reshape(layers, -1, TILES, ROWS, 128)


def unview(t, shape):
    layers, rows, columns = shape
    return t.reshape(layers, rows // 8, columns // 128, 8, 128).transpose(0, 1, 3, 2, 4).reshape(shape)


def place():
    me = lax.axis_index("dp")
    return me, me // 2, me % 2


def is_down(t):
    return (t % 3) // 2


def source(t):
    i = 2 * (t // 3) + t % 3
    return i // PARTS, i % PARTS, t // 3


def bits(a):
    return ((8, 1, 4, 2), (4, 1, 8, 2))[a]


def by_kind(t, do):
    for down in (False, True):
        pl.when(is_down(t) == int(down))(functools.partial(do, down))


def bit(k, b):
    return (k // b) % 2


def flip(k, b):
    return k + (1 - 2 * bit(k, b)) * b


def copy_to(src, dst, send, recv, chip, core):
    return pltpu.make_async_remote_copy(src_ref=src, dst_ref=dst, send_sem=send, recv_sem=recv, device_id={"dp": 2 * chip + core}, device_id_type=MESH)


def sum_kernel(gate, up, down, gate_out, up_out, down_out, norm, own, pair, slots, squares, parts, own_sem, pair_send, pair_recv, send, recv, norm_send, norm_recv):
    me, k, c = place()

    def load(t):
        def go(w_down):
            layer, part, down_part = source(t)
            for a in range(2):
                ref, layer_a, part_a = (down, a, down_part) if w_down else ((gate, up)[a], layer, part)
                at = pl.ds(part_a * PART, PART)
                copy_to(ref.at[layer_a, :, 1 - c, at], pair.at[t, a], pair_send.at[t, a], pair_recv.at[t, a], k, 1 - c).start()
                pltpu.make_async_copy(ref.at[layer_a, :, c, at], own.at[t, a], own_sem.at[t, a]).start()

        by_kind(t, go)

    lax.fori_loop(0, AHEAD, lambda t, _: load(t), None)
    squares[...] = jnp.zeros_like(squares)

    def await_slots(t, a, s):
        got = slots.at[t, a, pl.ds(START[s], COUNT[s])]
        pltpu.make_async_copy(got, got, recv.at[t, a, s]).wait()

    def total(t, a, s, chip):
        b = bits(a)
        so_far = own[t, a, chip].astype(jnp.float32) + pair[t, a, chip].astype(jnp.float32)
        for i in range(s):
            index = START[i]
            for j in range(i + 1, 4):
                index = index + bit(chip, b[j]) * 2 ** (3 - j)
            so_far = so_far + slots[t, a, index].astype(jnp.float32)
        return so_far

    def stage(t, a, s):
        b = bits(a)
        other = flip(k, b[s])
        if s == 0:
            pltpu.make_async_copy(own.at[t, a], own.at[t, a], own_sem.at[t, a]).wait()
            pltpu.make_async_copy(pair.at[t, a], pair.at[t, a], pair_recv.at[t, a]).wait()
        else:
            await_slots(t, a, s - 1)
        base = other
        for i in range(s + 1, 4):
            base = base - bit(other, b[i]) * b[i]

        def chip_of(j):
            chip = base
            for i in range(s + 1, 4):
                chip = chip + bit(j, 2 ** (3 - i)) * b[i]
            return chip

        def add(j, _):
            chip = chip_of(j)
            own[t, a, chip] = total(t, a, s, chip).astype(jnp.bfloat16)
            return 0

        def go(j, _):
            copy_to(own.at[t, a, chip_of(j)], slots.at[t, a, START[s] + j], send.at[t, a, s], recv.at[t, a, s], other, c).start()
            return 0

        lax.fori_loop(0, COUNT[s], add, 0)
        lax.fori_loop(0, COUNT[s], go, 0)

    def finish(t, a):
        await_slots(t, a, 3)
        g = total(t, a, 4, k).astype(jnp.bfloat16)

        def put(w_down):
            layer, part, down_part = source(t)
            out, layer, part = (down_out, a, down_part) if w_down else ((gate_out, up_out)[a], layer, part)
            out[layer, pl.ds(part * PART, PART)] = g

        by_kind(t, put)
        g = g.astype(jnp.float32)
        squares[...] += jnp.sum(g * g, axis=0)

    def step(now, _):
        pl.when(now + AHEAD < ROUNDS)(lambda: load(now + AHEAD))
        for s in range(5):
            t = now - SUM_LAG[s]

            @pl.when((t >= 0) & (t < ROUNDS))
            def _():
                for a in range(2):
                    if s < 4:
                        stage(t, a, s)
                    else:
                        finish(t, a)

        return 0

    lax.fori_loop(0, ROUNDS + SUM_LAG[4], step, 0)

    mine = parts.at[me]
    mine[...] = squares[...]

    def tell(i, _):
        to = (me + i) % 32
        pltpu.make_async_remote_copy(src_ref=squares, dst_ref=mine, send_sem=norm_send, recv_sem=norm_recv, device_id={"dp": to}, device_id_type=MESH).start()
        return 0

    lax.fori_loop(1, 32, tell, 0)
    others = parts.at[pl.ds(0, 31)]
    pltpu.make_async_copy(others, others, norm_recv).wait()
    norm[...] = jnp.sum(parts[...], axis=0)
    pltpu.make_async_copy(others, others, norm_send).wait()

    def drain(t, _):
        for a in range(2):
            pltpu.make_async_copy(pair.at[t, a], pair.at[t, a], pair_send.at[t, a]).wait()
            for s in range(4):
                sent = slots.at[t, a, pl.ds(START[s], COUNT[s])]
                pltpu.make_async_copy(sent, sent, send.at[t, a, s]).wait()
        return 0

    lax.fori_loop(0, ROUNDS, drain, 0)


def gather_kernel(gate_new, up_new, down_new, gate, up, down, own_sem, pair_send, pair_recv, send, recv):
    _, k, c = place()

    def block(w_down, t, a, chip, core, count=None):
        chip = chip if count is None else pl.ds(chip, count)
        layer, part, down_part = source(t)
        ref, layer, part = (down, a, down_part) if w_down else ((gate, up)[a], layer, part)
        return ref.at[layer, chip, core, pl.ds(part * PART, PART)]

    def chips(a, s, at):
        b = bits(a)[::-1]
        base = at
        for i in range(s):
            base = base - bit(at, b[i]) * b[i]

        def chip_of(j):
            chip = base
            for i in range(s):
                chip = chip + bit(j, 2**i) * b[i]
            return chip

        return chip_of

    def own_block(w_down, t, a):
        layer, part, down_part = source(t)
        ref, layer, part = (down_new, a, down_part) if w_down else ((gate_new, up_new)[a], layer, part)
        return pltpu.make_async_copy(ref.at[layer, pl.ds(part * PART, PART)], block(w_down, t, a, k, c), own_sem.at[t, a])

    def start_own(t, _):
        by_kind(t, lambda w_down: [own_block(w_down, t, a).start() for a in range(2)] and None)
        return 0

    lax.fori_loop(0, ROUNDS, start_own, 0)

    def stage(w_down, t, a, s):
        if s == 0:
            own_block(w_down, t, a).wait()
            fresh, count = chips(a, 0, k), 1
        else:
            count = 2 ** (s - 1)
            got = block(w_down, t, a, 0, 0, count)
            pltpu.make_async_copy(got, got, recv.at[t, a, s - 1]).wait()
            fresh = chips(a, s - 1, flip(k, bits(a)[4 - s]))
        if s < 4:
            of, other = chips(a, s, k), flip(k, bits(a)[3 - s])

            def go(j, _):
                one = block(w_down, t, a, of(j), c)
                copy_to(one, one, send.at[t, a, s], recv.at[t, a, s], other, c).start()
                return 0

            lax.fori_loop(0, 2**s, go, 0)

        def share(j, _):
            one = block(w_down, t, a, fresh(j), c)
            copy_to(one, one, pair_send.at[t, a], pair_recv.at[t, a], k, 1 - c).start()
            return 0

        lax.fori_loop(0, count, share, 0)

    def step(now, _):
        for s in range(5):
            t = now - GATHER_LAG[s]

            @pl.when((t >= 0) & (t < ROUNDS))
            def _():
                def go(w_down):
                    for a in range(2):
                        stage(w_down, t, a, s)

                by_kind(t, go)

        return 0

    lax.fori_loop(0, ROUNDS + GATHER_LAG[4], step, 0)

    def drain(t, _):
        for a in range(2):
            for sems, s in ((pair_recv.at[t, a], 4), (pair_send.at[t, a], 4), *((send.at[t, a, s], s) for s in range(4))):
                size = gate.at[0, pl.ds(0, 2**s), 0, pl.ds(0, PART)]
                pltpu.make_async_copy(size, size, sems).wait()
        return 0

    lax.fori_loop(0, ROUNDS, drain, 0)


def update_kernel(count, g, norm, w, m, v, w_new, m_new, v_new, w_now, m_now, v_now, got, put):
    me, _, _ = place()
    units = [(i, layer) for i in range(3) for layer in range(2)]

    def moves(u, inward):
        i, layer = units[u]
        come = ((w[i].at[layer, me], w_now), (m[i].at[layer], m_now), (v[i].at[layer], v_now))
        leave = (w_new[i].at[layer], m_new[i].at[layer], v_new[i].at[layer])
        if inward:
            return [pltpu.make_async_copy(there, here.at[u], got.at[u, n]) for n, (there, here) in enumerate(come)]
        return [pltpu.make_async_copy(here.at[u], there, put.at[u, n]) for n, ((_, here), there) in enumerate(zip(come, leave, strict=True))]

    for u in range(6):
        for one in moves(u, True):
            one.start()
    squares = jnp.full((ROWS, 128), jnp.sum(norm[...]), jnp.float32)
    factor = jnp.minimum(1.0, 0.5 * lax.rsqrt(squares / count + 1e-30))
    for u, (i, layer) in enumerate(units):
        for one in moves(u, True):
            one.wait()

        def go(j, _):
            at = pl.ds(j * PART, PART)
            gradient = g[i][layer, at].astype(jnp.float32) * factor
            w_now[u, at], m_now[u, at], v_now[u, at] = adamw(w_now[u, at].astype(jnp.float32), m_now[u, at], v_now[u, at], gradient)
            return 0

        lax.fori_loop(0, PARTS, go, 0)
        for one in moves(u, False):
            one.start()
    for u in range(6):
        for one in moves(u, False):
            one.wait()


def store_kernel(*refs):
    copies = [pltpu.make_async_copy(refs[i].at[layer], refs[3 + i].at[layer], refs[6].at[i, layer]) for i in range(3) for layer in range(2)]
    for one in copies:
        one.start()
    for one in copies:
        one.wait()


def adamw(w, m, v, g):
    m = 0.9 * m + 0.1 * g
    v = 0.95 * v + 0.05 * g * g
    step = m * lax.rsqrt(v + 1e-8) + 0.1 * w
    return (w - 0.02 * step).astype(jnp.bfloat16), m, v


def solution(mesh):
    hbm, vmem, fixed = (pl.BlockSpec(memory_space=one) for one in (pl.ANY, pltpu.VMEM, pltpu.HBM))
    dma = pltpu.SemaphoreType.DMA
    small = pltpu.CompilerParams(vmem_limit_bytes=1 << 20)
    params = pltpu.CompilerParams(has_side_effects=True, vmem_limit_bytes=67043328)

    def step(*arrays):
        terms, weights, m, v = (arrays[i : i + 3] for i in (0, 3, 6, 9))
        tile = (ROWS, 128)
        terms = [view(t[0]).reshape(2, CHIPS, 2, TILES, *tile) for t in terms]
        *g, norm = pl.pallas_call(
            sum_kernel,
            out_shape=[*[jax.ShapeDtypeStruct((2, TILES, *tile), jnp.bfloat16)] * 3, jax.ShapeDtypeStruct(tile, jnp.float32)],
            in_specs=[hbm] * 3,
            out_specs=[vmem] * 4,
            scratch_shapes=[
                pltpu.VMEM((ROUNDS, 2, CHIPS, PART, *tile), jnp.bfloat16),
                pltpu.VMEM((ROUNDS, 2, CHIPS, PART, *tile), jnp.bfloat16),
                pltpu.VMEM((ROUNDS, 2, 15, PART, *tile), jnp.bfloat16),
                pltpu.VMEM(tile, jnp.float32),
                pltpu.VMEM((32, *tile), jnp.float32),
                dma((ROUNDS, 2)),
                dma((ROUNDS, 2)),
                dma((ROUNDS, 2)),
                dma((ROUNDS, 2, 4)),
                dma((ROUNDS, 2, 4)),
                dma,
                dma,
            ],
            compiler_params=params,
        )(*terms)
        count = 32 * sum(one.size for one in m)

        def update(*refs):
            threes = [refs[i : i + 3] for i in (0, 4, 7, 10, 13, 16, 19)]
            update_kernel(count, threes[0], refs[3], *threes[1:], *refs[22:])

        mine = (2, TILES, *tile)
        *new, m0, m1, m2, v0, v1, v2 = pl.pallas_call(
            update,
            out_shape=[jax.ShapeDtypeStruct(mine, jnp.bfloat16)] * 3 + [jax.ShapeDtypeStruct(mine, jnp.float32)] * 6,
            in_specs=[vmem] * 4 + [fixed] * 9,
            out_specs=[fixed] * 9,
            scratch_shapes=[
                pltpu.VMEM((6, TILES, *tile), jnp.bfloat16),
                pltpu.VMEM((6, TILES, *tile), jnp.float32),
                pltpu.VMEM((6, TILES, *tile), jnp.float32),
                dma((6, 3)),
                dma((6, 3)),
            ],
        )(*g, norm, *(view(one) for one in weights), *(view(one)[:, 0] for one in (*m, *v)))
        whole = pl.pallas_call(
            gather_kernel,
            out_shape=[jax.ShapeDtypeStruct((2, CHIPS, 2, TILES, *tile), jnp.bfloat16)] * 3,
            in_specs=[vmem] * 3,
            out_specs=[hbm] * 3,
            scratch_shapes=[
                dma((ROUNDS, 2)),
                dma((ROUNDS, 2)),
                dma((ROUNDS, 2)),
                dma((ROUNDS, 2, 4)),
                dma((ROUNDS, 2, 4)),
            ],
            compiler_params=pltpu.CompilerParams(has_side_effects=True, vmem_limit_bytes=4 << 20),
        )(*new)
        whole = pl.pallas_call(store_kernel, out_shape=[jax.ShapeDtypeStruct(one.shape, one.dtype) for one in whole], in_specs=[hbm] * 3, out_specs=[hbm] * 3, scratch_shapes=[dma((3, 2))], compiler_params=small)(*whole)
        whole = [unview(one, w.shape) for one, w in zip(whole, weights, strict=True)]
        moments = [unview(one, like.shape) for one, like in zip((m0, m1, m2, v0, v1, v2), (*m, *v), strict=True)]
        return (*whole, *moments)

    all_of, cut = P(None, None, None), P(None, "dp", None)
    return jax.shard_map(
        step,
        mesh=mesh,
        in_specs=(P(("rep", "dp"), None, None, None),) * 3 + (all_of,) * 3 + (cut,) * 6,
        out_specs=(P("rep", None, None),) * 3 + (P("rep", "dp", None),) * 6,
        check_vma=False,
    )
```

time: 412 us -> 363 us (0.88)
  local copies, waits for them, and re-layouts: 29.2 us -> 3.02 us
  other arithmetic: 18.7 us -> 0 us
    unnamed x27 -> x6, local copies, waits for them, and re-layouts: 23.9 us -> 3.02 us
    pallas_call x1, Pallas kernels: 180 us -> 162 us  [step(): pl.pallas_call(gather_kernel, out_shape=[jax.ShapeDtypeStruct((2, CHIPS,...]
    pallas_call x1 -> x3, Pallas kernels: 182 us -> 197 us  [the longest x1 177 us: step(): pl.pallas_call(sum_kernel, out_shape=[*[jax.ShapeDtypeStruct((2, TILES, *...]
    reshape x2 -> x0, other arithmetic: 7.89 us -> none  [unview(): t.reshape(layers, rows // 8, columns // 128, 8, 128)]
    mul x8 -> x0, other arithmetic: 5.94 us -> none  [the longest x2 3.11 us: step(): g = [one.astype(jnp.float32) * factor for one in split(summed)]]
where the time goes in v2:
time: 363 us; the launch traced here: 362 us
  Pallas kernels  359 us (99%)
    pallas_call x1, Pallas kernels, step(): pl.pallas_call(sum_kernel, out_shape=[*[jax.ShapeDtypeStruct((2, TILES, *...  177 us
    pallas_call x1, Pallas kernels, step(): pl.pallas_call(gather_kernel, out_shape=[jax.ShapeDtypeStruct((2, CHIPS,...  162 us
    pallas_call x1, Pallas kernels, step(): pl.pallas_call(store_kernel, out_shape=[jax.ShapeDtypeStruct(one.shape, o...  13.4 us

profile of v2, /device:TPU:0, one launch (start us, length us, event | category | flops | bytes accessed | tf_op | source)
XLA Modules:
  0.0 362.4 jit_solution(16981824784677878192)
XLA Ops:
  0.6 177.0 %shard_map.187 = (bf16[2,104,8,128]{3,2,1,0:T(8,128)(2,1)}, bf16[2,104,8,128]{3,2,1,0:T(8,128)(2,1)}, bf16[2,104,8,128]{3,2,1,0:T(8,128)(2,1)}, f32[8,128]{1,0:T(8,128)}) custom-call(bf16[2,16,2,104,8,128]{5,4,3,2,1,0:T(8,128)(2,1)} %bitcast.105, bf16[2,16,2,104,8,128]{5,4,3,2,1,0:T(8,128)(2,1)} %bitcast.106, bf16[2,16,2,104,8,128]{5,4,3,2,1,0:T(8,128)(2,1)} %bitcast.107), custom_call_target="tpu_custom_call" | custom-call | tf_op jit(solution)/shard_map/pallas_call | solution.py:328
  177.6 6.6 %shard_map.188 = (bf16[2,104,8,128]{3,2,1,0:T(8,128)(2,1)}, bf16[2,104,8,128]{3,2,1,0:T(8,128)(2,1)}, bf16[2,104,8,128]{3,2,1,0:T(8,128)(2,1)}, f32[2,104,8,128]...) custom-call(bf16[2,104,8,128]{3,2,1,0:T(8,128)(2,1)} %get-tuple-elem, ...), custom_call_target="tpu_custom_call" | custom-call | tf_op jit(solution)/shard_map/pallas_call | solution.py:356
  184.2 0.0 copy-start
  184.3 1.0 copy-done
  185.3 0.0 copy-start.1
  185.3 1.0 copy-done.1
  186.3 0.0 copy-start.2
  186.3 1.0 copy-done.2
  187.3 161.8 %shard_map.189 = (bf16[2,16,2,104,8,128]{5,4,3,2,1,0:T(8,128)(2,1)S(1)}, bf16[2,16,2,104,8,128]{5,4,3,2,1,0:T(8,128)(2,1)S(1)}, bf16[2,16,2,104,8,128]{5,4,3,2,1,0:T(8,128)(2,1)S(1)}) custom-call(bf16[2,104,8,128]{3,2,1,0:T(8,128)(2,1)S(1)} %copy-done, bf16[2,104,8,128]{3,2,1,0:T(8,128)(2,1)S(1)} %copy-done.1, bf16[2,104,8,128]{3,2,1,0:T(8,128)(2,1)S(1)} %copy-done.2), custom_call_target="tpu_custom_call" | custom-call | tf_op jit(solution)/shard_map/pallas_call | solution.py:369
  349.0 13.4 %shard_map.190 = (bf16[2,16,2,104,8,128]{5,4,3,2,1,0:T(8,128)(2,1)}, bf16[2,16,2,104,8,128]{5,4,3,2,1,0:T(8,128)(2,1)}, bf16[2,16,2,104,8,128]{5,4,3,2,1,0:T(8,128)(2,1)}) custom-call(bf16[2,16,2,104,8,128]{5,4,3,2,1,0:T(8,128)(2,1)S(1)} %get-tuple-element.35.refs_0_, bf16[2,16,2,104,8,128]{5,4,3,2,1,0:T(8,128)(2,1)S(1)} %get-tuple-element.36.refs_1_, ...), custom_call_target="tpu_custom_call" | custom-call | tf_op jit(solution)/shard_map/pallas_call | solution.py:383
Async XLA Ops:
  184.2 1.0 copy-start
  185.3 1.0 copy-start.1
  186.3 1.0 copy-start.2

commit v3 on v2

--- a/solution.py
+++ b/solution.py
@@ -14,6 +14,7 @@
 ROUNDS = 3 * PARTS
 START, COUNT = (0, 8, 12, 14), (8, 4, 2, 1)
 AHEAD = 3
+LIMIT = 12
 SUM_LAG = (0, 1, 2, 3, 4)
 GATHER_LAG = (0, 1, 2, 3, 4)
 
@@ -179,8 +180,26 @@
     lax.fori_loop(0, ROUNDS, drain, 0)
 
 
-def gather_kernel(gate_new, up_new, down_new, gate, up, down, own_sem, pair_send, pair_recv, send, recv):
-    _, k, c = place()
+def unit_loads(sources, buffers, sems, i, layer):
+    u = 2 * i + layer
+    return [pltpu.make_async_copy(one[i].at[layer], here.at[u], sems.at[u, n]) for n, (one, here) in enumerate(zip(sources, buffers, strict=True))]
+
+
+def factor_of(norm, count):
+    squares = jnp.full((ROWS, 128), jnp.sum(norm[...]), jnp.float32)
+    return jnp.minimum(1.0, 0.5 * lax.rsqrt(squares / count + 1e-30))
+
+
+UNITS = ((0, 0), (1, 0), (2, 0), (2, 1), (0, 1), (1, 1))
+
+
+def gather_kernel(size, norm, g, w, m, v, gate, up, down, g_now, w_now, m_now, v_now, got, own_sem, pair_send, pair_recv, send, recv):
+    me, k, c = place()
+    sources, buffers = (g, [one.at[:, me] for one in w], m, v), (g_now, w_now, m_now, v_now)
+    for i, layer in UNITS:
+        for one in unit_loads(sources, buffers, got, i, layer):
+            one.start()
+    factor = factor_of(norm, size)
 
     def block(w_down, t, a, chip, core, count=None):
         chip = chip if count is None else pl.ds(chip, count)
@@ -202,26 +221,40 @@
 
         return chip_of
 
+    def own_part(w_down, t, a):
+        layer, part, down_part = source(t)
+        i, layer, part = (2, a, down_part) if w_down else (a, layer, part)
+        return i, layer, part, w_now.at[2 * i + layer, pl.ds(part * PART, PART)]
+
     def own_block(w_down, t, a):
-        layer, part, down_part = source(t)
-        ref, layer, part = (down_new, a, down_part) if w_down else ((gate_new, up_new)[a], layer, part)
-        return pltpu.make_async_copy(ref.at[layer, pl.ds(part * PART, PART)], block(w_down, t, a, k, c), own_sem.at[t, a])
-
-    def start_own(t, _):
-        by_kind(t, lambda w_down: [own_block(w_down, t, a).start() for a in range(2)] and None)
-        return 0
-
-    lax.fori_loop(0, ROUNDS, start_own, 0)
+        return pltpu.make_async_copy(own_part(w_down, t, a)[3], block(w_down, t, a, k, c), own_sem.at[t, a])
+
+    def renew(w_down, t, a):
+        i, layer, part, mine = own_part(w_down, t, a)
+
+        @pl.when(part == 0)
+        def _():
+            for one in unit_loads(sources, buffers, got, i, layer):
+                one.wait()
+
+        u, at = 2 * i + layer, pl.ds(part * PART, PART)
+        gradient = g_now[u, at].astype(jnp.float32) * factor
+        mine[...] = adamw(mine[...].astype(jnp.float32), m_now[u, at], v_now[u, at], gradient)[0]
 
     def stage(w_down, t, a, s):
         if s == 0:
+            mine = own_part(w_down, t, a)[3]
+            own_block(w_down, t, a).start()
+            there = block(w_down, t, a, k, c)
+            copy_to(mine, there, send.at[t, a, 0], recv.at[t, a, 0], flip(k, bits(a)[3]), c).start()
+            copy_to(mine, there, pair_send.at[t, a], pair_recv.at[t, a], k, 1 - c).start()
+            return
+        if s == 1:
             own_block(w_down, t, a).wait()
-            fresh, count = chips(a, 0, k), 1
-        else:
-            count = 2 ** (s - 1)
-            got = block(w_down, t, a, 0, 0, count)
-            pltpu.make_async_copy(got, got, recv.at[t, a, s - 1]).wait()
-            fresh = chips(a, s - 1, flip(k, bits(a)[4 - s]))
+        count = 2 ** (s - 1)
+        size = block(w_down, t, a, 0, 0, count)
+        pltpu.make_async_copy(size, size, recv.at[t, a, s - 1]).wait()
+        fresh = chips(a, s - 1, flip(k, bits(a)[4 - s]))
         if s < 4:
             of, other = chips(a, s, k), flip(k, bits(a)[3 - s])
 
@@ -246,6 +279,9 @@
             @pl.when((t >= 0) & (t < ROUNDS))
             def _():
                 def go(w_down):
+                    if s == 0:
+                        for a in range(2):
+                            renew(w_down, t, a)
                     for a in range(2):
                         stage(w_down, t, a, s)
 
@@ -265,46 +301,31 @@
     lax.fori_loop(0, ROUNDS, drain, 0)
 
 
-def update_kernel(count, g, norm, w, m, v, w_new, m_new, v_new, w_now, m_now, v_now, got, put):
-    me, _, _ = place()
-    units = [(i, layer) for i in range(3) for layer in range(2)]
-
-    def moves(u, inward):
-        i, layer = units[u]
-        come = ((w[i].at[layer, me], w_now), (m[i].at[layer], m_now), (v[i].at[layer], v_now))
-        leave = (w_new[i].at[layer], m_new[i].at[layer], v_new[i].at[layer])
-        if inward:
-            return [pltpu.make_async_copy(there, here.at[u], got.at[u, n]) for n, (there, here) in enumerate(come)]
-        return [pltpu.make_async_copy(here.at[u], there, put.at[u, n]) for n, ((_, here), there) in enumerate(zip(come, leave, strict=True))]
-
-    for u in range(6):
-        for one in moves(u, True):
+def store_kernel(size, norm, g, m, v, whole, w_out, m_out, v_out, g_now, m_now, v_now, got, put, put_whole):
+    sources, buffers = (g, m, v), (g_now, m_now, v_now)
+    for i, layer in UNITS:
+        for one in unit_loads(sources, buffers, got, i, layer):
             one.start()
-    squares = jnp.full((ROWS, 128), jnp.sum(norm[...]), jnp.float32)
-    factor = jnp.minimum(1.0, 0.5 * lax.rsqrt(squares / count + 1e-30))
-    for u, (i, layer) in enumerate(units):
-        for one in moves(u, True):
+    stores = [pltpu.make_async_copy(whole[i].at[layer], w_out[i].at[layer], put_whole.at[2 * i + layer]) for i, layer in UNITS]
+    for one in stores:
+        one.start()
+    factor = factor_of(norm, size)
+    for i, layer in UNITS:
+        for one in unit_loads(sources, buffers, got, i, layer):
             one.wait()
+        u = 2 * i + layer
 
         def go(j, _):
             at = pl.ds(j * PART, PART)
-            gradient = g[i][layer, at].astype(jnp.float32) * factor
-            w_now[u, at], m_now[u, at], v_now[u, at] = adamw(w_now[u, at].astype(jnp.float32), m_now[u, at], v_now[u, at], gradient)
+            gradient = g_now[u, at].astype(jnp.float32) * factor
+            _, m_now[u, at], v_now[u, at] = adamw(jnp.zeros((), jnp.float32), m_now[u, at], v_now[u, at], gradient)
             return 0
 
         lax.fori_loop(0, PARTS, go, 0)
-        for one in moves(u, False):
-            one.start()
-    for u in range(6):
-        for one in moves(u, False):
-            one.wait()
-
-
-def store_kernel(*refs):
-    copies = [pltpu.make_async_copy(refs[i].at[layer], refs[3 + i].at[layer], refs[6].at[i, layer]) for i in range(3) for layer in range(2)]
-    for one in copies:
-        one.start()
-    for one in copies:
+        for n, (here, there) in enumerate(((m_now, m_out), (v_now, v_out))):
+            stores.append(pltpu.make_async_copy(here.at[u], there[i].at[layer], put.at[u, n]))
+            stores[-1].start()
+    for one in stores:
         one.wait()
 
 
@@ -315,10 +336,13 @@
     return (w - 0.02 * step).astype(jnp.bfloat16), m, v
 
 
+def stay(one):
+    return pltpu.with_memory_space_constraint(one, pltpu.HBM)
+
+
 def solution(mesh):
-    hbm, vmem, fixed = (pl.BlockSpec(memory_space=one) for one in (pl.ANY, pltpu.VMEM, pltpu.HBM))
+    hbm, vmem = (pl.BlockSpec(memory_space=one) for one in (pl.ANY, pltpu.VMEM))
     dma = pltpu.SemaphoreType.DMA
-    small = pltpu.CompilerParams(vmem_limit_bytes=1 << 20)
     params = pltpu.CompilerParams(has_side_effects=True, vmem_limit_bytes=67043328)
 
     def step(*arrays):
@@ -348,41 +372,47 @@
         )(*terms)
         count = 32 * sum(one.size for one in m)
 
-        def update(*refs):
-            threes = [refs[i : i + 3] for i in (0, 4, 7, 10, 13, 16, 19)]
-            update_kernel(count, threes[0], refs[3], *threes[1:], *refs[22:])
+        def gather(norm, *refs):
+            threes = [refs[i : i + 3] for i in (0, 3, 6, 9)]
+            gather_kernel(count, norm, *threes, *refs[12:])
+
+        def store(norm, *refs):
+            threes = [refs[i : i + 3] for i in range(0, 21, 3)]
+            store_kernel(count, norm, *threes, *refs[21:])
 
         mine = (2, TILES, *tile)
-        *new, m0, m1, m2, v0, v1, v2 = pl.pallas_call(
-            update,
-            out_shape=[jax.ShapeDtypeStruct(mine, jnp.bfloat16)] * 3 + [jax.ShapeDtypeStruct(mine, jnp.float32)] * 6,
-            in_specs=[vmem] * 4 + [fixed] * 9,
-            out_specs=[fixed] * 9,
-            scratch_shapes=[
-                pltpu.VMEM((6, TILES, *tile), jnp.bfloat16),
-                pltpu.VMEM((6, TILES, *tile), jnp.float32),
-                pltpu.VMEM((6, TILES, *tile), jnp.float32),
-                dma((6, 3)),
-                dma((6, 3)),
-            ],
-        )(*g, norm, *(view(one) for one in weights), *(view(one)[:, 0] for one in (*m, *v)))
+        blocks = [jax.ShapeDtypeStruct((2, CHIPS, 2, TILES, *tile), jnp.bfloat16)] * 3
+        m, v = ([view(one)[:, 0] for one in them] for them in (m, v))
+        narrow, wide = pltpu.VMEM((6, TILES, *tile), jnp.bfloat16), pltpu.VMEM((6, TILES, *tile), jnp.float32)
         whole = pl.pallas_call(
-            gather_kernel,
-            out_shape=[jax.ShapeDtypeStruct((2, CHIPS, 2, TILES, *tile), jnp.bfloat16)] * 3,
-            in_specs=[vmem] * 3,
+            gather,
+            out_shape=blocks,
+            in_specs=[vmem] + [hbm] * 12,
             out_specs=[hbm] * 3,
             scratch_shapes=[
+                narrow,
+                narrow,
+                wide,
+                wide,
+                dma((6, 4)),
                 dma((ROUNDS, 2)),
                 dma((ROUNDS, 2)),
                 dma((ROUNDS, 2)),
                 dma((ROUNDS, 2, 4)),
                 dma((ROUNDS, 2, 4)),
             ],
-            compiler_params=pltpu.CompilerParams(has_side_effects=True, vmem_limit_bytes=4 << 20),
-        )(*new)
-        whole = pl.pallas_call(store_kernel, out_shape=[jax.ShapeDtypeStruct(one.shape, one.dtype) for one in whole], in_specs=[hbm] * 3, out_specs=[hbm] * 3, scratch_shapes=[dma((3, 2))], compiler_params=small)(*whole)
+            compiler_params=pltpu.CompilerParams(has_side_effects=True, vmem_limit_bytes=LIMIT << 20),
+        )(norm, *map(stay, (*g, *(view(one) for one in weights), *m, *v)))
+        *whole, m0, m1, m2, v0, v1, v2 = pl.pallas_call(
+            store,
+            out_shape=blocks + [jax.ShapeDtypeStruct(mine, jnp.float32)] * 6,
+            in_specs=[vmem] + [hbm] * 12,
+            out_specs=[hbm] * 9,
+            scratch_shapes=[narrow, wide, wide, dma((6, 3)), dma((6, 2)), dma((6,))],
+            compiler_params=pltpu.CompilerParams(vmem_limit_bytes=LIMIT << 20),
+        )(norm, *map(stay, (*g, *m, *v)), *whole)
         whole = [unview(one, w.shape) for one, w in zip(whole, weights, strict=True)]
-        moments = [unview(one, like.shape) for one, like in zip((m0, m1, m2, v0, v1, v2), (*m, *v), strict=True)]
+        moments = [unview(one, like.shape) for one, like in zip((m0, m1, m2, v0, v1, v2), arrays[6:], strict=True)]
         return (*whole, *moments)
 
     all_of, cut = P(None, None, None), P(None, "dp", None)

time: 363 us -> 357 us (0.983)
    pallas_call x3 -> x2, Pallas kernels: 182 us -> 179 us  [the longest x1 162 us: step(): pl.pallas_call(gather, out_shape=blocks, in_specs=[vmem] + [hbm] * 12, ou...]
where the time goes in v3:
time: 357 us
  Pallas kernels  356 us (100%)
    pallas_call x1, Pallas kernels, step(): pl.pallas_call(sum_kernel, out_shape=[*[jax.ShapeDtypeStruct((2, TILES, *...  177 us
    pallas_call x1, Pallas kernels, step(): pl.pallas_call(gather, out_shape=blocks, in_specs=[vmem] + [hbm] * 12, ou...  162 us
    pallas_call x1, Pallas kernels, step(): pl.pallas_call(store, out_shape=blocks + [jax.ShapeDtypeStruct(mine, jnp....  16.7 us

profile of v3, /device:TPU:0, one launch (start us, length us, event | category | flops | bytes accessed | tf_op | source)
XLA Modules:
  0.0 357.1 jit_solution(10551467328895220997)
XLA Ops:
  0.6 177.0 %shard_map.187 = (bf16[2,104,8,128]{3,2,1,0:T(8,128)(2,1)}, bf16[2,104,8,128]{3,2,1,0:T(8,128)(2,1)}, bf16[2,104,8,128]{3,2,1,0:T(8,128)(2,1)}, f32[8,128]{1,0:T(8,128)}) custom-call(bf16[2,16,2,104,8,128]{5,4,3,2,1,0:T(8,128)(2,1)} %bitcast.105, bf16[2,16,2,104,8,128]{5,4,3,2,1,0:T(8,128)(2,1)} %bitcast.106, bf16[2,16,2,104,8,128]{5,4,3,2,1,0:T(8,128)(2,1)} %bitcast.107), custom_call_target="tpu_custom_call" | custom-call | tf_op jit(solution)/shard_map/pallas_call | solution.py:352
  177.6 0.0 copy-start
  177.6 0.7 copy-done
  178.3 162.1 %shard_map.188 = (bf16[2,16,2,104,8,128]{5,4,3,2,1,0:T(8,128)(2,1)S(1)}, bf16[2,16,2,104,8,128]{5,4,3,2,1,0:T(8,128)(2,1)S(1)}, bf16[2,16,2,104,8,128]{5,4,3,2,1,0:T(8,128)(2,1)S(1)}) custom-call(f32[8,128]{1,0:T(8,128)S(1)} %copy-done, bf16[2,104,8,128]{3,2,1,0:T(8,128)(2,1)} %get-tuple-element.26.refs_0_, ...), custom_call_target="tpu_custom_call" | custom-call | tf_op jit(solution)/shard_map/pallas_call | solution.py:387
  340.4 16.7 %shard_map.189 = (bf16[2,16,2,104,8,128]{5,4,3,2,1,0:T(8,128)(2,1)}, bf16[2,16,2,104,8,128]{5,4,3,2,1,0:T(8,128)(2,1)}, bf16[2,16,2,104,8,128]{5,4,3,2,1,0:T(8,1...) custom-call(f32[8,128]{1,0:T(8,128)S(1)} %copy-done, ...), custom_call_target="tpu_custom_call" | custom-call | tf_op jit(solution)/shard_map/pallas_call | solution.py:406
Async XLA Ops:
  177.6 0.7 copy-start

commit v4 on v3

--- a/solution.py
+++ b/solution.py
@@ -15,7 +15,7 @@
 START, COUNT = (0, 8, 12, 14), (8, 4, 2, 1)
 AHEAD = 3
 LIMIT = 12
-SUM_LAG = (0, 1, 2, 3, 4)
+SUM_LAG = (0, 2, 3, 4, 5)
 GATHER_LAG = (0, 1, 2, 3, 4)
 
 
@@ -122,8 +122,14 @@
             copy_to(own.at[t, a, chip_of(j)], slots.at[t, a, START[s] + j], send.at[t, a, s], recv.at[t, a, s], other, c).start()
             return 0
 
-        lax.fori_loop(0, COUNT[s], add, 0)
-        lax.fori_loop(0, COUNT[s], go, 0)
+        def add_and_go(j, _):
+            add(j, 0)
+            go(j - 1, 0)
+            return 0
+
+        add(0, 0)
+        lax.fori_loop(1, COUNT[s], add_and_go, 0)
+        go(COUNT[s] - 1, 0)
 
     def finish(t, a):
         await_slots(t, a, 3)

time: 357 us -> 360 us (level)
  no operation moved by 1% of the time
where the time goes in v4:
time: 360 us
  Pallas kernels  358 us (99%)
    pallas_call x1, Pallas kernels, step(): pl.pallas_call(sum_kernel, out_shape=[*[jax.ShapeDtypeStruct((2, TILES, *...  178 us
    pallas_call x1, Pallas kernels, step(): pl.pallas_call(gather, out_shape=blocks, in_specs=[vmem] + [hbm] * 12, ou...  163 us
    pallas_call x1, Pallas kernels, step(): pl.pallas_call(store, out_shape=blocks + [jax.ShapeDtypeStruct(mine, jnp....  16.7 us

profile of v4, /device:TPU:0, one launch (start us, length us, event | category | flops | bytes accessed | tf_op | source)
XLA Modules:
  0.0 359.6 jit_solution(6954244516696215773)
XLA Ops:
  0.6 178.2 %shard_map.187 = (bf16[2,104,8,128]{3,2,1,0:T(8,128)(2,1)}, bf16[2,104,8,128]{3,2,1,0:T(8,128)(2,1)}, bf16[2,104,8,128]{3,2,1,0:T(8,128)(2,1)}, f32[8,128]{1,0:T(8,128)}) custom-call(bf16[2,16,2,104,8,128]{5,4,3,2,1,0:T(8,128)(2,1)} %bitcast.105, bf16[2,16,2,104,8,128]{5,4,3,2,1,0:T(8,128)(2,1)} %bitcast.106, bf16[2,16,2,104,8,128]{5,4,3,2,1,0:T(8,128)(2,1)} %bitcast.107), custom_call_target="tpu_custom_call" | custom-call | tf_op jit(solution)/shard_map/pallas_call | solution.py:358
  178.8 0.0 copy-start
  178.9 0.7 copy-done
  179.5 163.3 %shard_map.188 = (bf16[2,16,2,104,8,128]{5,4,3,2,1,0:T(8,128)(2,1)S(1)}, bf16[2,16,2,104,8,128]{5,4,3,2,1,0:T(8,128)(2,1)S(1)}, bf16[2,16,2,104,8,128]{5,4,3,2,1,0:T(8,128)(2,1)S(1)}) custom-call(f32[8,128]{1,0:T(8,128)S(1)} %copy-done, bf16[2,104,8,128]{3,2,1,0:T(8,128)(2,1)} %get-tuple-element.26.refs_0_, ...), custom_call_target="tpu_custom_call" | custom-call | tf_op jit(solution)/shard_map/pallas_call | solution.py:393
  342.9 16.7 %shard_map.189 = (bf16[2,16,2,104,8,128]{5,4,3,2,1,0:T(8,128)(2,1)}, bf16[2,16,2,104,8,128]{5,4,3,2,1,0:T(8,128)(2,1)}, bf16[2,16,2,104,8,128]{5,4,3,2,1,0:T(8,1...) custom-call(f32[8,128]{1,0:T(8,128)S(1)} %copy-done, ...), custom_call_target="tpu_custom_call" | custom-call | tf_op jit(solution)/shard_map/pallas_call | solution.py:412
Async XLA Ops:
  178.8 0.7 copy-start
